TPU v7x, 32 devices: a whole 2x2x4 slice. The times are simulated.
32 devices in a mesh: grp: 4 (over y, x), chan: 8 (over z, core).
Axes of the slice: x: 2, y: 2, z: 4, core: 2. Of those that a mesh axis runs over, the one named last changes fastest.
Arguments:
- visibility: float32 [1024, 32768], P('chan', 'grp'), may hold values from -6 to 6
- interference_mask: int32 [1024, 16384], P(None, ('grp', 'chan')), may hold values from 0 to 1
- valid_time_count: int32 [512], P(('grp', 'chan')), may hold values from 8 to 32
- fit_modes: float32 [1024, 32], P('grp'), may hold values from -1 to 1
Outputs:
- residual_vis: float32 [1024, 32768], P('chan', 'grp')
All inputs are finite; a program needn't handle non-finite values.
Results may differ from a plain program's by a relative error of at most 0.0003.
Values sent between devices are 32-bit elements; how exact they have to be, the bound alone decides.
A program may use at most 128 MiB of HBM per device.

v0:
```python
import jax
import jax.numpy as jnp
from jax import lax
from jax.sharding import PartitionSpec as P

damping = 0.1


def fit_weight(interference_mask, valid_time_count):
    antenna_pairs_list = valid_time_count.shape[0]
    sample_values = interference_mask.shape[1] // antenna_pairs_list
    projection_sums = lax.broadcasted_iota(jnp.int32, (antenna_pairs_list, sample_values), 1)
    within_range = (
        (projection_sums < valid_time_count[:, None])
        .astype(jnp.float32)
        .reshape(1, antenna_pairs_list * sample_values)
    )
    return (1.0 - interference_mask.astype(jnp.float32)) * within_range


def solve_normal(normal_matrix, target_signal):
    span_length = normal_matrix.shape[0]
    trailing = normal_matrix
    columns = []
    for position in range(span_length):
        column = trailing[:, 0] / jnp.sqrt(trailing[0, 0])
        columns.append(column)
        trailing = trailing[1:, 1:] - column[1:, None, :] * column[None, 1:, :]
    remains = target_signal
    forward = []
    for position in range(span_length):
        column = columns[position]
        current = remains[0] / column[0][None, :]
        forward.append(current)
        remains = remains[1:] - column[1:, None, :] * current[None]
    solution_values = [None] * span_length
    for position in reversed(range(span_length)):
        column = columns[position]
        current = forward[position]
        if position + 1 < span_length:
            later_rows = jnp.stack(solution_values[position + 1 :], 0)
            current = current - jnp.sum(column[1:, None, :] * later_rows, axis=0)
        solution_values[position] = current / column[0][None, :]
    return jnp.stack(solution_values, 0)


def solve_amplitudes(spectral_templates, assigned_rows, sample_weight, antenna_pairs_list):
    channel_count, span_length = spectral_templates.shape
    sample_values = sample_weight.shape[1] // antenna_pairs_list
    pairs = (spectral_templates[:, :, None] * spectral_templates[:, None, :]).reshape(
        channel_count, span_length * span_length
    )
    normal_matrix = lax.dot_general(
        pairs,
        sample_weight,
        (((0,), (0,)), ((), ())),
        precision=lax.Precision.HIGHEST,
        preferred_element_type=jnp.float32,
    )
    normal_matrix = normal_matrix.reshape(
        span_length, span_length, antenna_pairs_list * sample_values
    )
    normal_matrix = (
        normal_matrix + damping * jnp.eye(span_length, dtype=normal_matrix.dtype)[:, :, None]
    )
    weighted_values = assigned_rows.reshape(
        channel_count, antenna_pairs_list, 2, sample_values
    ) * sample_weight.reshape(channel_count, antenna_pairs_list, 1, sample_values)
    weighted_values = weighted_values.reshape(channel_count, antenna_pairs_list * 2 * sample_values)
    template_projection = lax.dot_general(
        spectral_templates,
        weighted_values,
        (((0,), (0,)), ((), ())),
        precision=lax.Precision.HIGHEST,
        preferred_element_type=jnp.float32,
    )
    target_signal = (
        template_projection.reshape(span_length, antenna_pairs_list, 2, sample_values)
        .transpose(0, 2, 1, 3)
        .reshape(span_length, 2, antenna_pairs_list * sample_values)
    )
    solution_values = solve_normal(normal_matrix, target_signal)
    return (
        solution_values.reshape(span_length, 2, antenna_pairs_list, sample_values)
        .transpose(0, 2, 1, 3)
        .reshape(span_length, antenna_pairs_list * 2 * sample_values)
    )


def per_device(visibility, interference_mask, valid_time_count, fit_modes):
    spectral_templates = lax.all_gather(fit_modes, "grp", axis=0, tiled=True)
    assigned_rows = lax.all_to_all(visibility, "chan", split_axis=1, concat_axis=0, tiled=True)
    antenna_pairs_list = valid_time_count.shape[0]
    sample_weight = fit_weight(interference_mask, valid_time_count)
    mode_amplitudes = solve_amplitudes(
        spectral_templates, assigned_rows, sample_weight, antenna_pairs_list
    )
    local_rows = visibility.shape[0]
    local_basis = lax.dynamic_slice_in_dim(
        spectral_templates, lax.axis_index("chan") * local_rows, local_rows, 0
    )
    model = jnp.dot(
        local_basis,
        lax.all_gather(mode_amplitudes, "chan", axis=1, tiled=True),
        precision=lax.Precision.HIGHEST,
        preferred_element_type=jnp.float32,
    )
    return visibility - model


def solution(mesh):
    placed = (P("chan", "grp"), P(None, ("grp", "chan")), P(("grp", "chan")), P("grp", None))
    return jax.shard_map(
        per_device, mesh=mesh, in_specs=placed, out_specs=P("chan", "grp"), check_vma=False
    )
```

profile of v0, /device:TPU:0, one launch (start us, length us, event | category | flops | bytes accessed | tf_op | source)
XLA Modules:
  0.0 204.1 jit_solution(10742631934232733337)
XLA Ops:
  6.5 5.6 %copy.41 = f32[128,8192]{0,1:T(8,128)} copy(f32[128,8192]{1,0:T(8,128)} %param.4) | data formatting | bytes 8388608 | tf_op args[0]
  12.1 6.5 %all-to-all-start = ((f32[128,8,1024]{0,2,1:T(8,128)}), f32[128,8,1024]{0,2,1:T(8,128)}, u32[]{:S(2)}, u32[]{:S(2)}) async-start(f32[128,8,1024]{0,2,1:T(8,128)} %bitcast.362), calls=%async_computation | async-start | bytes 8388608 | tf_op jit(solution)/shard_map/all_to_all | solution.py:92
  18.8 8.5 %all_gather.6 = f32[1024,32]{0,1:T(8,128)S(1)} all-gather(f32[256,32]{0,1:T(8,128)S(1)} %copy-done.17), channel_id=1, replica_groups=mesh['grp'=4,'chan'=8] {'grp'}, dimensions={0}, use_global_device_ids=true | all-gather | bytes 163840 | tf_op jit(solution)/shard_map/all_gather | solution.py:91
  27.3 1.8 copy.43
  29.1 1.8 subtract_multiply_fusion
  30.9 6.7 %fusion.6 = f32[32,32,512]{2,1,0:T(8,128)S(1)} fusion(f32[1024,512]{0,1:T(8,128)S(1)} %subtract_multiply_fusion, f32[1024,32]{0,1:T(8,128)S(1)} %all_gather.6, f32[32,32]{1,0:T(8,128)S(1)} %fusion.13), kind=kOutput, calls=%fused_computation.16 | convolution fusion | flops 6444023808 | bytes 4329472 | tf_op jit(solution)/shard_map/dot_general | solution.py:53
  53.5 2.5 %mul.536 = f32[1024,16,2,32]{0,3,2,1:T(8,128)} broadcast(f32[1024,16,32]{0,2,1:T(8,128)S(1)} %bitcast.364), dimensions={0,1,3} | broadcast | bytes 6291456 | tf_op jit(solution)/shard_map/mul | solution.py:66
  56.0 5.3 %copy.44 = f32[1024,1024]{1,0:T(8,128)} copy(f32[1024,1024]{0,1:T(8,128)} %bitcast.363) | data formatting | bytes 8388608 | tf_op jit(solution)/shard_map/mul | solution.py:66
  61.4 51.3 %all-to-all-done = f32[128,8,1024]{0,2,1:T(8,128)} async-done(((f32[128,8,1024]{0,2,1:T(8,128)}), f32[128,8,1024]{0,2,1:T(8,128)}, u32[]{:S(2)}, u32[]{:S(2)}) %all-to-all-start) | async-done | bytes 4194336 | tf_op jit(solution)/shard_map/all_to_all | solution.py:92
  112.7 5.3 %copy.42 = f32[8,128,1024]{2,1,0:T(8,128)} copy(f32[8,128,1024]{1,2,0:T(8,128)} %bitcast.1) | data formatting | bytes 8388608 | tf_op jit(solution)/shard_map/all_to_all | solution.py:92
  118.0 4.4 %bitcast_multiply_fusion = f32[1024,1024]{1,0:T(8,128)S(1)} fusion(f32[1024,1024]{1,0:T(8,128)} %copy.44, f32[8,128,1024]{2,1,0:T(8,128)} %copy.42), kind=kLoop, calls=%fused_computation.3 | loop fusion | flops 1048576 | bytes 12582912 | tf_op jit(solution)/shard_map/mul | solution.py:66
  122.4 2.6 %convolution_bitcast_fusion = f32[32,1024]{1,0:T(8,128)S(1)} fusion(f32[1024,1024]{1,0:T(8,128)S(1)} %bitcast_multiply_fusion, f32[1024,32]{0,1:T(8,128)S(1)} %all_gather.6), kind=kOutput, calls=%fused_computation.18 | convolution fusion | flops 402653184 | bytes 4456448 | tf_op jit(solution)/shard_map/dot_general | solution.py:70
  128.3 0.7 slice_subtract_fusion.58
  130.6 0.7 fusion.46
  132.0 0.7 fusion.45
  132.8 0.7 constant_dynamic-update-slice_fusion.4
  133.6 1.3 constant_dynamic-update-slice_fusion.10
  137.9 0.8 multiply_reduce_fusion.25
  138.7 1.3 constant_dynamic-update-slice_fusion.17
  144.2 0.8 multiply_reduce_fusion.24
  145.0 0.7 constant_dynamic-update-slice_fusion.25
  146.4 0.7 constant_dynamic-update-slice_fusion.34
  147.9 0.7 constant_dynamic-update-slice_fusion.44
  149.7 0.7 constant_dynamic-update-slice_fusion.67
  150.7 0.7 constant_dynamic-update-slice_fusion.80
  151.6 0.7 constant_dynamic-update-slice_fusion.94
  152.6 0.7 constant_dynamic-update-slice_fusion.109
  153.8 0.7 constant_dynamic-update-slice_fusion.142
  155.9 0.7 constant_dynamic-update-slice_fusion.179
  166.6 1.3 reshape.1023
  167.9 21.3 %all-gather.2.cloned.1.call-done = f32[32,8192]{1,0:T(8,128)} async-done(((f32[32,1024]{1,0:T(8,128)}), f32[32,8192]{1,0:T(8,128)}) %all-gather.2.cloned.1.call-update) | async-done | bytes 1048592 | tf_op jit(solution)/shard_map/all_gather | solution.py:104
  189.3 8.0 %convolution_subtract_fusion = f32[128,8192]{1,0:T(8,128)} fusion(f32[128,8192]{1,0:T(8,128)} %param.4, f32[32,8192]{1,0:T(8,128)} %all-gather.2.cloned.1.call-done, f32[1024,32]{0,1:T(8,128)S(1)} %all_gather.6, s32[]{:T(128)S(6)} %select_n.3), kind=kOutput, calls=%fused_computation | convolution fusion | flops 403701760 | bytes 9453572 | tf_op jit(solution)/shard_map/dot_general | solution.py:102
  (938 shorter events, 40.5 us)
Async XLA Ops:
  12.1 6.6 %copy-start.56 = (s32[16]{0:T(128)S(1)}, s32[16]{0:T(128)}, u32[]{:S(2)}) copy-start(s32[16]{0:T(128)} %param.6) | copy-start | bytes 196
  12.1 6.7 %copy-start.17 = (f32[256,32]{0,1:T(8,128)S(1)}, f32[256,32]{0,1:T(8,128)}, u32[]{:S(2)}) copy-start(f32[256,32]{0,1:T(8,128)} %param.7) | copy-start | bytes 98308
  12.1 15.2 %copy-start = (s32[1024,512]{1,0:T(8,128)S(1)}, s32[1024,512]{1,0:T(8,128)}, u32[]{:S(2)}) copy-start(s32[1024,512]{1,0:T(8,128)} %param.5) | copy-start | bytes 6291460
  12.1 100.6 %all-to-all-start = ((f32[128,8,1024]{0,2,1:T(8,128)}), f32[128,8,1024]{0,2,1:T(8,128)}, u32[]{:S(2)}, u32[]{:S(2)}) async-start(f32[128,8,1024]{0,2,1:T(8,128)} %bitcast.362), calls=%async_computation | async-start | bytes 8388608 | tf_op jit(solution)/shard_map/all_to_all | solution.py:92
  18.6 170.7 %all-gather.2.cloned.1.call-start = ((), (), s32[]{:S(2)}) async-start(), calls=%async_computation.1 | async-start | bytes 1179648 | tf_op jit(solution)/shard_map/all_gather | solution.py:104
  44.0 82.0 %copy-start.19 = (f32[1,512]{1,0:T(1,128)}, f32[1,512]{1,0:T(1,128)S(1)}, u32[]{:S(2)}) copy-start(f32[1,512]{1,0:T(1,128)S(1)} %slice.1010) | copy-start | bytes 6148
  44.0 82.1 %copy-start.21 = (f32[1,512]{1,0:T(1,128)}, f32[1,512]{1,0:T(1,128)S(1)}, u32[]{:S(2)}) copy-start(f32[1,512]{1,0:T(1,128)S(1)} %slice.1017) | copy-start | bytes 6148
  44.0 82.2 %copy-start.23 = (f32[1,512]{1,0:T(1,128)}, f32[1,512]{1,0:T(1,128)S(1)}, u32[]{:S(2)}) copy-start(f32[1,512]{1,0:T(1,128)S(1)} %slice.1024) | copy-start | bytes 6148
  44.0 82.3 %copy-start.25 = (f32[1,512]{1,0:T(1,128)}, f32[1,512]{1,0:T(1,128)S(1)}, u32[]{:S(2)}) copy-start(f32[1,512]{1,0:T(1,128)S(1)} %slice.1031) | copy-start | bytes 6148
  44.1 82.4 %copy-start.27 = (f32[1,512]{1,0:T(1,128)}, f32[1,512]{1,0:T(1,128)S(1)}, u32[]{:S(2)}) copy-start(f32[1,512]{1,0:T(1,128)S(1)} %slice.1038) | copy-start | bytes 6148
  44.1 82.5 %copy-start.29 = (f32[1,512]{1,0:T(1,128)}, f32[1,512]{1,0:T(1,128)S(1)}, u32[]{:S(2)}) copy-start(f32[1,512]{1,0:T(1,128)S(1)} %slice.1045) | copy-start | bytes 6148
  44.1 82.6 %copy-start.31 = (f32[1,512]{1,0:T(1,128)}, f32[1,512]{1,0:T(1,128)S(1)}, u32[]{:S(2)}) copy-start(f32[1,512]{1,0:T(1,128)S(1)} %slice.1052) | copy-start | bytes 6148
  44.1 82.7 %copy-start.33 = (f32[1,512]{1,0:T(1,128)}, f32[1,512]{1,0:T(1,128)S(1)}, u32[]{:S(2)}) copy-start(f32[1,512]{1,0:T(1,128)S(1)} %slice.1059) | copy-start | bytes 6148
  44.1 82.8 %copy-start.34 = (f32[1,512]{1,0:T(1,128)}, f32[1,512]{1,0:T(1,128)S(1)}, u32[]{:S(2)}) copy-start(f32[1,512]{1,0:T(1,128)S(1)} %slice.1066) | copy-start | bytes 6148
  44.2 82.8 %copy-start.35 = (f32[1,512]{1,0:T(1,128)}, f32[1,512]{1,0:T(1,128)S(1)}, u32[]{:S(2)}) copy-start(f32[1,512]{1,0:T(1,128)S(1)} %slice.1073) | copy-start | bytes 6148
  44.2 82.9 %copy-start.36 = (f32[1,512]{1,0:T(1,128)}, f32[1,512]{1,0:T(1,128)S(1)}, u32[]{:S(2)}) copy-start(f32[1,512]{1,0:T(1,128)S(1)} %slice.1080) | copy-start | bytes 6148
  44.2 82.9 %copy-start.37 = (f32[1,512]{1,0:T(1,128)}, f32[1,512]{1,0:T(1,128)S(1)}, u32[]{:S(2)}) copy-start(f32[1,512]{1,0:T(1,128)S(1)} %slice.1087) | copy-start | bytes 6148
  44.2 83.0 %copy-start.38 = (f32[1,512]{1,0:T(1,128)}, f32[1,512]{1,0:T(1,128)S(1)}, u32[]{:S(2)}) copy-start(f32[1,512]{1,0:T(1,128)S(1)} %slice.1094) | copy-start | bytes 6148
  44.2 83.0 %copy-start.39 = (f32[1,512]{1,0:T(1,128)}, f32[1,512]{1,0:T(1,128)S(1)}, u32[]{:S(2)}) copy-start(f32[1,512]{1,0:T(1,128)S(1)} %slice.1101) | copy-start | bytes 6148
  44.3 83.1 %copy-start.40 = (f32[1,512]{1,0:T(1,128)}, f32[1,512]{1,0:T(1,128)S(1)}, u32[]{:S(2)}) copy-start(f32[1,512]{1,0:T(1,128)S(1)} %slice.1108) | copy-start | bytes 6148
  44.3 83.2 %copy-start.41 = (f32[1,512]{1,0:T(1,128)}, f32[1,512]{1,0:T(1,128)S(1)}, u32[]{:S(2)}) copy-start(f32[1,512]{1,0:T(1,128)S(1)} %slice.1115) | copy-start | bytes 6148
  52.1 3.9 %copy-start.9 = (f32[3,3,512]{2,1,0:T(4,128)}, f32[3,3,512]{2,1,0:T(4,128)S(1)}, u32[]{:S(2)}) copy-start(f32[3,3,512]{2,1,0:T(4,128)S(1)} %slice_subtract_fusion.52) | copy-start | bytes 55300
  134.9 18.7 %copy-start.42 = (f32[1,512]{1,0:T(1,128)S(1)}, f32[1,512]{1,0:T(1,128)}, u32[]{:S(2)}) copy-start(f32[1,512]{1,0:T(1,128)} %copy-done.41) | copy-start | bytes 6148
  150.6 11.4 %copy-start.32 = (f32[1,512]{1,0:T(1,128)S(1)}, f32[1,512]{1,0:T(1,128)}, u32[]{:S(2)}) copy-start(f32[1,512]{1,0:T(1,128)} %copy-done.31) | copy-start | bytes 6148
  152.4 10.1 %copy-start.30 = (f32[1,512]{1,0:T(1,128)S(1)}, f32[1,512]{1,0:T(1,128)}, u32[]{:S(2)}) copy-start(f32[1,512]{1,0:T(1,128)} %copy-done.29) | copy-start | bytes 6148
  153.6 9.4 %copy-start.28 = (f32[1,512]{1,0:T(1,128)S(1)}, f32[1,512]{1,0:T(1,128)}, u32[]{:S(2)}) copy-start(f32[1,512]{1,0:T(1,128)} %copy-done.27) | copy-start | bytes 6148
  154.8 8.7 %copy-start.26 = (f32[1,512]{1,0:T(1,128)S(1)}, f32[1,512]{1,0:T(1,128)}, u32[]{:S(2)}) copy-start(f32[1,512]{1,0:T(1,128)} %copy-done.25) | copy-start | bytes 6148
  156.6 7.3 %copy-start.24 = (f32[1,512]{1,0:T(1,128)S(1)}, f32[1,512]{1,0:T(1,128)}, u32[]{:S(2)}) copy-start(f32[1,512]{1,0:T(1,128)} %copy-done.23) | copy-start | bytes 6148
  157.8 6.7 %copy-start.22 = (f32[1,512]{1,0:T(1,128)S(1)}, f32[1,512]{1,0:T(1,128)}, u32[]{:S(2)}) copy-start(f32[1,512]{1,0:T(1,128)} %copy-done.21) | copy-start | bytes 6148
  158.9 6.1 %copy-start.20 = (f32[1,512]{1,0:T(1,128)S(1)}, f32[1,512]{1,0:T(1,128)}, u32[]{:S(2)}) copy-start(f32[1,512]{1,0:T(1,128)} %copy-done.19) | copy-start | bytes 6148
  160.8 4.9 %copy-start.18 = (f32[16,32]{1,0:T(8,128)S(1)}, f32[16,32]{1,0:T(8,128)}, u32[]{:S(2)}) copy-start(f32[16,32]{1,0:T(8,128)} %div.867) | copy-start | bytes 6148
  162.5 3.8 %copy-start.12 = (f32[1,2,16,32]{3,2,1,0:T(8,128)S(1)}, f32[1,2,16,32]{3,2,1,0:T(8,128)}, u32[]{:S(2)}) copy-start(f32[1,2,16,32]{3,2,1,0:T(8,128)} %stack.183) | copy-start | bytes 12292
  (27 other events, 49.7 us)
Sparse Core Ops, SparseCore 0:
  168.1 21.1 all-gather.1
where the time goes:
time: 205 us; the launch traced here: 204 us
  waiting for transfers between devices  72.7 us (35%)
  local copies, waits for them, and re-layouts  49.4 us (24%)
  other arithmetic  32.3 us (16%)
  between operations  17.4 us (8%)
  matrix products  17.3 us (8%)
  blocking collectives  8.45 us (4%)
  starting transfers between devices  6.53 us (3%)
    all_to_all x1, waiting for transfers between devices, per_device(): lax.all_to_all(visibility, 'chan', split_axis=1, concat_axis=0, tiled=True)  51.3 us
    all_gather x1, waiting for transfers between devices, per_device(): lax.all_gather(mode_amplitudes, 'chan', axis=1, tiled=True)  21.3 us
    unnamed x578, local copies, waits for them, and re-layouts  16.9 us
    unnamed x28, other arithmetic  14.1 us
    all_gather x1, blocking collectives, per_device(): spectral_templates = lax.all_gather(fit_modes, 'grp', axis=0, tiled=True)  8.45 us
    dot_general x1, matrix products, per_device(): jnp.dot(local_basis, lax.all_gather(mode_amplitudes, 'chan', axis=1, tile...  8 us
    mul x2, local copies, waits for them, and re-layouts, solve_amplitudes(): assigned_rows.reshape(channel_count, antenna_pairs_list, 2, sample_values)  7.88 us
    slice x32, local copies, waits for them, and re-layouts, solve_normal(): current = remains[0] / column[0][None, :]  7.51 us
  transfers between devices with their start and end apart: 2, of which 2 were waited for; matrix products, arithmetic and copies ran while one was open for 16% of the time, Pallas kernels for 0%

commit v1 on v0

v1 whole, which is shorter than its diff:
```python
import functools

import jax
import jax.numpy as jnp
from jax import lax
from jax.experimental import pallas as pl
from jax.experimental.pallas import tpu as pltpu
from jax.sharding import PartitionSpec as P

damping = 0.1
LANES = 128
VMEM = pl.BlockSpec(memory_space=pltpu.VMEM)
MESH = pl.DeviceIdType.MESH


def factor_kernel(mt_ref, mask_ref, valid_ref, spread_ref, l_ref, inv_ref, w_ref, hi_ref, mid_ref, lo_ref):
    modes, freqs = mt_ref.shape
    columns = mask_ref.shape[1]
    for j in range(columns // LANES):
        part = slice(j * LANES, (j + 1) * LANES)
        w = (1.0 - mask_ref[:, part].astype(jnp.float32)) * valid_ref[:, part]
        w_ref[:, 2 * j * LANES : 2 * (j + 1) * LANES] = jnp.dot(
            w.astype(jnp.bfloat16), spread_ref[...], preferred_element_type=jnp.float32
        ).astype(jnp.bfloat16)

    def split(i, carry):
        pair = mt_ref[...] * mt_ref[pl.ds(i, 1), :]
        rows = pl.ds(pl.multiple_of(i * modes, modes), modes)
        hi = pair.astype(jnp.bfloat16)
        rest = pair - hi.astype(jnp.float32)
        mid = rest.astype(jnp.bfloat16)
        hi_ref[rows, :] = hi
        mid_ref[rows, :] = mid
        lo_ref[rows, :] = (rest - mid.astype(jnp.float32)).astype(jnp.bfloat16)
        return carry

    lax.fori_loop(0, modes, split, 0)
    tile, group = 2 * LANES, 8

    def gram(step, carry):
        cols = pl.ds(pl.multiple_of(step // (modes // group) * tile, tile), tile)
        first = step % (modes // group)
        rows = pl.ds(pl.multiple_of(first * group * modes, group * modes), group * modes)
        w = w_ref[:, cols]
        total = jnp.dot(lo_ref[rows, :], w, preferred_element_type=jnp.float32)
        total += jnp.dot(mid_ref[rows, :], w, preferred_element_type=jnp.float32)
        total += jnp.dot(hi_ref[rows, :], w, preferred_element_type=jnp.float32)
        l_ref[pl.ds(first * group, group), :, cols] = total.reshape(group, modes, tile)
        return carry

    lax.fori_loop(0, 2 * columns // tile * (modes // group), gram, 0)
    width = 4 * LANES

    def cholesky(step, carry):
        cols = pl.ds(pl.multiple_of(step * width, width), width)
        for k in range(modes):
            low = k // 8 * 8
            row = lax.broadcasted_iota(jnp.int32, (modes - low, width), 0) + low
            acc = l_ref[k, low:, cols] + jnp.where(row == k, damping, 0.0)
            for m in range(k):
                acc = acc - l_ref[m, low:, cols] * l_ref[m, k : k + 1, cols]
            inv = 1.0 / jnp.sqrt(acc[k - low : k - low + 1])
            inv_ref[k : k + 1, cols] = inv
            l_ref[k, low:, cols] = acc * inv
        return carry

    lax.fori_loop(0, 2 * columns // width, cholesky, 0)


def fit_kernel(chips, vis_ref, mask_ref, mt_ref, spread_ref, valid_ref, l_ref, inv_ref, out_ref,
               give, keep, take, sums, come, sems):
    me = lax.axis_index("chan")
    chip, core = me // 2, me % 2
    modes, width = inv_ref.shape
    columns = mask_ref.shape[2]
    barrier = pltpu.get_barrier_semaphore()
    pl.semaphore_signal(barrier, inc=1, device_id={"chan": chip * 2 + 1 - core}, device_id_type=MESH)
    for d in range(1, chips):
        peer = lax.rem(chip + d, chips)
        pl.semaphore_signal(barrier, inc=1, device_id={"chan": peer * 2 + core}, device_id_type=MESH)
    pl.semaphore_wait(barrier, chips)

    def copy(stage, src, dst, slot, peer, at):
        return pltpu.make_async_remote_copy(
            src_ref=src, dst_ref=dst, send_sem=sems.at[2 * stage, slot], recv_sem=sems.at[2 * stage + 1, at],
            device_id={"chan": peer}, device_id_type=MESH)

    mate = chip * 2 + 1 - core

    def project(owner, dst, slot):
        for j in range(columns // LANES):
            w = 1.0 - mask_ref[owner, :, j * LANES : (j + 1) * LANES].astype(jnp.float32)
            w = jnp.dot(w.astype(jnp.bfloat16), spread_ref[...], preferred_element_type=jnp.float32)
            at = pl.multiple_of(owner * width + 2 * j * LANES, 2 * LANES)
            v = vis_ref[:, pl.ds(at, 2 * LANES)] * w
            dst[slot, :, 2 * j * LANES : 2 * (j + 1) * LANES] = jnp.dot(
                mt_ref[...], v, precision=lax.Precision.HIGHEST, preferred_element_type=jnp.float32)

    def theirs(d, carry):
        slot = lax.rem(chip + d, chips)
        project(slot * 2 + 1 - core, give, slot)
        copy(0, give.at[slot], take.at[slot], slot, mate, slot).start()
        return carry

    lax.fori_loop(1, chips + 1, theirs, 0)

    def mine(d, carry):
        slot = lax.rem(chip + d, chips)
        project(slot * 2 + core, keep, slot)
        return carry

    lax.fori_loop(1, chips + 1, mine, 0)
    for d in range(1, chips + 1):
        slot = lax.rem(chip + d, chips)
        copy(0, give.at[slot], take.at[slot], slot, mate, slot).wait()
        if d < chips:
            sums[slot] = keep[slot] + take[slot]
            copy(1, sums.at[slot], come.at[chip], slot, slot * 2 + core, chip).start()
    total = keep[chip] + take[chip]
    for d in range(1, chips):
        slot = lax.rem(chip + d, chips)
        copy(1, sums.at[slot], come.at[slot], slot, slot * 2 + core, slot).wait()
        total = total + come[slot]
    take[chip] = total * valid_ref[...]

    part = 2 * LANES

    def solve(step, carry):
        cols = pl.ds(pl.multiple_of(step * part, part), part)
        row = lax.broadcasted_iota(jnp.int32, (modes, part), 0)
        left = take[chip, :, cols]
        groups = [left[g * 8 : (g + 1) * 8] for g in range(modes // 8)]
        ys = []
        for k in range(modes):
            low = k // 8
            y = groups[low][k % 8 : k % 8 + 1] * inv_ref[k : k + 1, cols]
            ys.append(y)
            for g in range(low, modes // 8):
                groups[g] = groups[g] - l_ref[k, g * 8 : (g + 1) * 8, cols] * y
        row = lax.broadcasted_iota(jnp.int32, (8, part), 0)
        xs = [jnp.zeros((8, part), jnp.float32) for _ in range(modes // 8)]
        for k in reversed(range(modes)):
            low = k // 8
            acc = l_ref[k, low * 8 : (low + 1) * 8, cols] * xs[low]
            for g in range(low + 1, modes // 8):
                acc = acc + l_ref[k, g * 8 : (g + 1) * 8, cols] * xs[g]
            x = (ys[k] - jnp.sum(acc, axis=0, keepdims=True)) * inv_ref[k : k + 1, cols]
            xs[low] = jnp.where(row == k % 8, x, xs[low])
        for g in range(modes // 8):
            out_ref[me, g * 8 : (g + 1) * 8, cols] = xs[g]
        return carry

    lax.fori_loop(0, width // part, solve, 0)

    def spread(slot):
        block = out_ref.at[slot * 2 + core]
        return copy(3, block, block, slot, mate, slot)

    for d in range(1, chips):
        slot = lax.rem(chip + d, chips)
        copy(2, out_ref.at[me], out_ref.at[me], slot, slot * 2 + core, chip).start()
    spread(chip).start()
    for d in range(1, chips):
        slot = lax.rem(chip + d, chips)
        block = out_ref.at[slot * 2 + core]
        copy(2, block, block, slot, slot * 2 + core, slot).wait_recv()
        spread(slot).start()
    for d in range(1, chips):
        slot = lax.rem(chip + d, chips)
        copy(2, out_ref.at[me], out_ref.at[me], slot, slot * 2 + core, chip).wait_send()
    for slot in range(chips):
        block = out_ref.at[slot * 2 + 1 - core]
        spread(slot).wait_send()
        copy(3, block, block, slot, mate, slot).wait_recv()


def residual_kernel(vis_ref, modes_ref, coef_ref, out_ref):
    width = coef_ref.shape[2]
    for j in range(coef_ref.shape[0]):
        cols = slice(j * width, (j + 1) * width)
        out_ref[:, cols] = vis_ref[:, cols] - jnp.dot(
            modes_ref[...], coef_ref[j], precision=lax.Precision.HIGHEST, preferred_element_type=jnp.float32)


def per_device(chan, visibility, interference_mask, valid_time_count, fit_modes):
    rows, all_columns = visibility.shape
    freqs, columns = interference_mask.shape
    modes = fit_modes.shape[1]
    base = valid_time_count.shape[0]
    times = columns // base
    width = 2 * columns
    chips = chan // 2
    flags = lax.all_to_all(interference_mask.reshape(chan, rows, columns), "chan", 0, 0)
    table = lax.all_gather(fit_modes, "grp", axis=0, tiled=True)
    local = lax.dynamic_slice_in_dim(table, lax.axis_index("chan") * rows, rows, 0)
    within = (lax.broadcasted_iota(jnp.int32, (base, times), 1) < valid_time_count[:, None]).astype(jnp.float32)
    valid = within.reshape(1, columns)
    valid_wide = jnp.broadcast_to(within[:, None, :], (base, 2, times)).reshape(1, width)
    source = lax.broadcasted_iota(jnp.int32, (LANES, 2 * LANES), 0)
    column = lax.broadcasted_iota(jnp.int32, (LANES, 2 * LANES), 1)
    spread = (source == column // (2 * times) * times + column % times).astype(jnp.bfloat16)
    f32 = jnp.float32
    factor, inverse = pl.pallas_call(
        factor_kernel,
        out_shape=(jax.ShapeDtypeStruct((modes, modes, width), f32), jax.ShapeDtypeStruct((modes, width), f32)),
        in_specs=[VMEM] * 4,
        out_specs=(VMEM, VMEM),
        scratch_shapes=[pltpu.VMEM((freqs, width), jnp.bfloat16)]
        + [pltpu.VMEM((modes * modes, freqs), jnp.bfloat16)] * 3,
        compiler_params=pltpu.CompilerParams(vmem_limit_bytes=40 << 20),
        cost_estimate=pl.CostEstimate(flops=20 * 10**9, bytes_accessed=8 << 20, transcendentals=0),
        name="factor",
    )(table.T, interference_mask, valid, spread)
    block = pltpu.VMEM((chips, modes, width), f32)
    coefficients = pl.pallas_call(
        functools.partial(fit_kernel, chips),
        out_shape=jax.ShapeDtypeStruct((chan, modes, width), f32),
        in_specs=[VMEM] * 7,
        out_specs=VMEM,
        scratch_shapes=[block] * 5 + [pltpu.SemaphoreType.DMA((8, chips))],
        compiler_params=pltpu.CompilerParams(
            collective_id=0, has_side_effects=True, vmem_limit_bytes=56 << 20),
        cost_estimate=pl.CostEstimate(flops=10**10, bytes_accessed=12 << 20, transcendentals=0),
        name="fit",
    )(visibility, flags, local.T, spread, valid_wide, factor, inverse)
    step = 2
    return pl.pallas_call(
        residual_kernel,
        grid=(chan // step,),
        out_shape=jax.ShapeDtypeStruct((rows, all_columns), f32),
        in_specs=[
            pl.BlockSpec((rows, step * width), lambda i: (0, i)),
            pl.BlockSpec((rows, modes), lambda i: (0, 0)),
            pl.BlockSpec((step, modes, width), lambda i: (i, 0, 0)),
        ],
        out_specs=pl.BlockSpec((rows, step * width), lambda i: (0, i)),
        name="residual",
    )(visibility, local, coefficients)


def solution(mesh):
    placed = (P("chan", "grp"), P(None, ("grp", "chan")), P(("grp", "chan")), P("grp", None))
    return jax.shard_map(
        functools.partial(per_device, mesh.shape["chan"]), mesh=mesh, in_specs=placed, out_specs=P("chan", "grp"),
        check_vma=False)
```

time: 205 us -> 101 us (0.49)
  Pallas kernels: 0 us -> 59.2 us
  waiting for transfers between devices: 72.7 us -> 19.1 us
  local copies, waits for them, and re-layouts: 49.4 us -> 5.01 us
  other arithmetic: 32.3 us -> 0.11 us
  between operations: 17.4 us -> 0.09 us
  matrix products: 17.3 us -> 0 us
  blocking collectives: 8.45 us -> 10.7 us
    pallas_call x0 -> x3, Pallas kernels: none -> 59.2 us  [the longest x1 37.9 us: per_device(): pl.pallas_call(functools.partial(fit_kernel, chips), out_shape=jax.ShapeD...]
    all_to_all x1, waiting for transfers between devices: 51.3 us -> 19.1 us  [per_device(): lax.all_to_all(interference_mask.reshape(chan, rows, columns), 'chan', 0, 0)]
    all_gather x1 -> x0, waiting for transfers between devices: 21.3 us -> none  [per_device(): lax.all_gather(mode_amplitudes, 'chan', axis=1, tiled=True)]
    dot_general x3 -> x0, matrix products: 17.3 us -> none  [the longest x1 8 us: per_device(): jnp.dot(local_basis, lax.all_gather(mode_amplitudes, 'chan', axis=1, tile...]
    unnamed x28 -> x0, other arithmetic: 14.1 us -> none
    unnamed x578 -> x13, local copies, waits for them, and re-layouts: 16.9 us -> 2.76 us
    slice x95 -> x0, local copies, waits for them, and re-layouts: 8.62 us -> none  [the longest x32 7.51 us: solve_normal(): current = remains[0] / column[0][None, :]]
    mul x2 -> x0, local copies, waits for them, and re-layouts: 7.88 us -> none  [solve_amplitudes(): assigned_rows.reshape(channel_count, antenna_pairs_list, 2, sample_values)]
  transfers between devices with their start and end apart: 2 -> 1, of which waited for: 2 -> 1; matrix products, arithmetic and copies ran while one was open for 16% -> 2% of each run, Pallas kernels for 0% -> 14%
where the time goes in v1:
time: 101 us
  Pallas kernels  59.2 us (59%)
  waiting for transfers between devices  19.1 us (19%)
  blocking collectives  10.7 us (11%)
  starting transfers between devices  6.5 us (6%)
  local copies, waits for them, and re-layouts  5.01 us (5%)
    pallas_call x1, Pallas kernels, per_device(): pl.pallas_call(functools.partial(fit_kernel, chips), out_shape=jax.ShapeD...  37.9 us
    all_to_all x1, waiting for transfers between devices, per_device(): lax.all_to_all(interference_mask.reshape(chan, rows, columns), 'chan', 0, 0)  19.1 us
    pallas_call x1, Pallas kernels, per_device(): pl.pallas_call(factor_kernel, out_shape=(jax.ShapeDtypeStruct((modes, mod...  14.2 us
    all_gather x1, blocking collectives, per_device(): table = lax.all_gather(fit_modes, 'grp', axis=0, tiled=True)  10.7 us
    pallas_call x1, Pallas kernels, per_device(): pl.pallas_call(residual_kernel, grid=(chan // step,), out_shape=jax.Shape...  7.21 us
    all_to_all x1, starting transfers between devices, per_device(): lax.all_to_all(interference_mask.reshape(chan, rows, columns), 'chan', 0, 0)  6.5 us
    unnamed x13, local copies, waits for them, and re-layouts  2.76 us
  transfers between devices with their start and end apart: 1, of which 1 were waited for; matrix products, arithmetic and copies ran while one was open for 2% of the time, Pallas kernels for 14%

profile of v1, /device:TPU:0, one launch (start us, length us, event | category | flops | bytes accessed | tf_op | source)
XLA Modules:
  0.0 100.7 jit_solution(8225244287686298124)
XLA Ops:
  0.0 0.0 copy-start
  0.0 0.0 copy-start.5
  0.0 0.0 copy-start.4
  0.0 6.5 %all-to-all-start = ((s32[8,128,512]{2,1,0:T(8,128)}), s32[8,128,512]{2,1,0:T(8,128)}, u32[]{:S(2)}, u32[]{:S(2)}) async-start(s32[8,128,512]{2,1,0:T(8,128)} %bitcast.4), calls=%async_computation | async-start | bytes 4194304 | tf_op jit(solution)/shard_map/all_to_all | solution.py:193
  6.5 0.0 copy-done.5
  6.5 0.1 fusion.1
  6.6 0.1 reshape.52.valid_ref
  6.7 0.7 reshape.51.valid_ref
  7.4 0.0 copy-done.4
  7.4 0.1 copy.5
  7.5 10.7 %all_gather.3 = f32[1024,32]{1,0:T(8,128)S(1)} all-gather(f32[256,32]{1,0:T(8,128)S(1)} %copy.5), channel_id=1, replica_groups=mesh['grp'=4,'chan'=8] {'grp'}, dimensions={0}, use_global_device_ids=true | all-gather | bytes 163840 | tf_op jit(solution)/shard_map/all_gather | solution.py:194
  18.2 0.7 copy.7.mt_ref
  18.9 0.2 copy.6.mt_ref
  19.1 0.6 constant_dynamic-slice_fusion.modes_ref
  19.7 0.0 copy-done
  19.7 0.0 copy-start.1
  19.8 14.2 %factor.1 = (f32[32,32,1024]{2,1,0:T(8,128)S(1)}, f32[32,1024]{1,0:T(8,128)S(1)}) custom-call(f32[32,1024]{1,0:T(8,128)S(1)} %copy.6.mt_ref, s32[1024,512]{1,0:T(8,128)S(1)} %copy-done, f32[1,512]{1,0:T(1,128)S(1)} %reshape.52.valid_ref, bf16[128,256]{1,0:T(8,128)(2,1)S(1)} %fusion.spread_ref), custom_call_target="tpu_custom_call" | custom-call | flops 20000000000 | bytes 8388608 | tf_op jit(solution)/shard_map/factor/pallas_call | solution.py:203
  33.9 0.0 copy-done.1
  33.9 0.0 copy-start.2
  34.0 2.0 %copy-done.2 = f32[32,32,1024]{2,1,0:T(8,128)} copy-done((f32[32,32,1024]{2,1,0:T(8,128)}, f32[32,32,1024]{2,1,0:T(8,128)S(1)}, u32[]{:S(2)}) %copy-start.2) | copy-done | bytes 4194328
  36.0 0.0 copy-start.3
  36.0 0.6 copy-done.3
  36.6 19.1 %all-to-all-done.mask_ref = s32[8,128,512]{2,1,0:T(8,128)} async-done(((s32[8,128,512]{2,1,0:T(8,128)}), s32[8,128,512]{2,1,0:T(8,128)}, u32[]{:S(2)}, u32[]{:S(2)}) %all-to-all-start) | async-done | bytes 2097184 | tf_op jit(solution)/shard_map/all_to_all | solution.py:193
  55.6 37.9 %fit.1.coef_ref = f32[8,32,1024]{2,1,0:T(8,128)} custom-call(f32[128,8192]{1,0:T(8,128)} %vis_ref.3, s32[8,128,512]{2,1,0:T(8,128)} %all-to-all-done.mask_ref, f32[32,128]{1,0:T(8,128)} %copy.7.mt_ref, bf16[128,256]{1,0:T(8,128)(2,1)} %copy-done.1, f32[1,1024]{1,0:T(1,128)} %reshape.51.valid_ref, f32[32,32,1024]{2,1,0:T(8,128)} %copy-done.2, ...), custom_call_target="tpu_custom_call" | custom-call | flops 10000000000 | bytes 12582912 | tf_op jit(solution)/shard_map/fit/pallas_call | solution.py:215
  93.5 7.2 %residual.1 = f32[128,8192]{1,0:T(8,128)} custom-call(f32[128,8192]{1,0:T(8,128)} %vis_ref.3, f32[128,32]{1,0:T(8,128)} %constant_dynamic-slice_fusion.modes_ref, f32[8,32,1024]{2,1,0:T(8,128)} %fit.1.coef_ref), custom_call_target="tpu_custom_call" | custom-call | tf_op jit(solution)/shard_map/residual/pallas_call | solution.py:227
  (6 shorter events, 0.1 us)
Async XLA Ops:
  0.0 19.7 %copy-start = (s32[1024,512]{1,0:T(8,128)S(1)}, s32[1024,512]{1,0:T(8,128)}, u32[]{:S(2)}) copy-start(s32[1024,512]{1,0:T(8,128)} %mask_ref.1) | copy-start | bytes 6291460
  0.0 6.5 %copy-start.5 = (s32[16]{0:T(128)S(1)}, s32[16]{0:T(128)}, u32[]{:S(2)}) copy-start(s32[16]{0:T(128)} %param.6) | copy-start | bytes 196
  0.0 7.4 %copy-start.4 = (f32[256,32]{0,1:T(8,128)S(1)}, f32[256,32]{0,1:T(8,128)}, u32[]{:S(2)}) copy-start(f32[256,32]{0,1:T(8,128)} %param.7) | copy-start | bytes 98308
  0.0 55.6 %all-to-all-start = ((s32[8,128,512]{2,1,0:T(8,128)}), s32[8,128,512]{2,1,0:T(8,128)}, u32[]{:S(2)}, u32[]{:S(2)}) async-start(s32[8,128,512]{2,1,0:T(8,128)} %bitcast.4), calls=%async_computation | async-start | bytes 4194304 | tf_op jit(solution)/shard_map/all_to_all | solution.py:193
  19.7 14.2 %copy-start.1 = (bf16[128,256]{1,0:T(8,128)(2,1)}, bf16[128,256]{1,0:T(8,128)(2,1)S(1)}, u32[]{:S(2)}) copy-start(bf16[128,256]{1,0:T(8,128)(2,1)S(1)} %fusion.spread_ref) | copy-start | bytes 196612
  33.9 2.0 %copy-start.2 = (f32[32,32,1024]{2,1,0:T(8,128)}, f32[32,32,1024]{2,1,0:T(8,128)S(1)}, u32[]{:S(2)}) copy-start(f32[32,32,1024]{2,1,0:T(8,128)S(1)} %get-tuple-element.7.l_ref) | copy-start | bytes 12582916
  36.0 0.6 copy-start.3

commit v2 on v1

--- a/solution.py
+++ b/solution.py
@@ -67,25 +67,72 @@
     lax.fori_loop(0, 2 * columns // width, cholesky, 0)
 
 
-def fit_kernel(chips, vis_ref, mask_ref, mt_ref, spread_ref, valid_ref, l_ref, inv_ref, out_ref,
-               give, keep, take, sums, come, sems):
-    me = lax.axis_index("chan")
+def fit_kernel(chips, groups, vis_hbm, mask_hbm, share_ref, spread_ref, valid_ref, wide_ref, out_ref, loc_ref,
+               vis_ref, own_ref, mask_ref, table, mt_all, w_ref, hi_ref, mid_ref, lo_ref, l_ref, inv_ref,
+               give, keep, take, sums, come, sems, mask_sems, table_sems, local_sems):
+    me, grp = lax.axis_index("chan"), lax.axis_index("grp")
     chip, core = me // 2, me % 2
+    turn = 1 - 2 * (2 * chip // chips)
     modes, width = inv_ref.shape
+    rows = vis_ref.shape[0]
     columns = mask_ref.shape[2]
+    share = share_ref.shape[1]
+    mate = chip * 2 + 1 - core
+
+    def other(d):
+        return lax.rem(chip + turn * d + chips, chips)
+
+    load_own = pltpu.make_async_copy(mask_hbm, own_ref, local_sems.at[0])
+    load_own.start()
     barrier = pltpu.get_barrier_semaphore()
-    pl.semaphore_signal(barrier, inc=1, device_id={"chan": chip * 2 + 1 - core}, device_id_type=MESH)
-    for d in range(1, chips):
-        peer = lax.rem(chip + d, chips)
-        pl.semaphore_signal(barrier, inc=1, device_id={"chan": peer * 2 + core}, device_id_type=MESH)
-    pl.semaphore_wait(barrier, chips)
+    for d in range(1, 2 * chips):
+        pl.semaphore_signal(barrier, inc=1, device_id={"chan": lax.rem(me + d, 2 * chips)}, device_id_type=MESH)
+    for d in range(1, groups):
+        pl.semaphore_signal(barrier, inc=1, device_id={"grp": lax.rem(grp + d, groups)}, device_id_type=MESH)
+    pl.semaphore_wait(barrier, 2 * chips + groups - 2)
+
+    def flags(peer, slot, at):
+        return pltpu.make_async_remote_copy(
+            src_ref=mask_hbm.at[pl.ds(pl.multiple_of(peer * rows, rows), rows)], dst_ref=mask_ref.at[slot],
+            send_sem=mask_sems.at[0, peer], recv_sem=mask_sems.at[1, at],
+            device_id={"chan": peer}, device_id_type=MESH)
+
+    def modes_copy(peer, slot):
+        return pltpu.make_async_remote_copy(
+            src_ref=share_ref, dst_ref=table.at[slot], send_sem=table_sems.at[0, peer],
+            recv_sem=table_sems.at[1, slot], device_id={"grp": peer}, device_id_type=MESH)
+
+    for d in range(1, groups):
+        modes_copy(lax.rem(grp + d, groups), grp).start()
+    flags(mate, me, me).start()
+    for d in range(1, chips):
+        flags(other(d) * 2 + core, me, me).start()
+        flags(other(d) * 2 + 1 - core, me, me).start()
+    load_vis = pltpu.make_async_copy(vis_hbm, vis_ref, local_sems.at[1])
+    load_vis.start()
+    load_mine = pltpu.make_async_copy(
+        mask_hbm.at[pl.ds(pl.multiple_of(me * rows, rows), rows)], mask_ref.at[me], local_sems.at[2])
+    load_mine.start()
+
+    table[grp] = share_ref[...]
+    for d in range(1, groups):
+        peer = lax.rem(grp + d, groups)
+        modes_copy(peer, peer).wait_recv()
+    for q in range(groups):
+        mt_all[:, q * share : (q + 1) * share] = table[q]
+    pick = lax.broadcasted_iota(jnp.int32, (groups * share, rows), 0)
+    pick = pick == lax.broadcasted_iota(jnp.int32, (groups * share, rows), 1) + me * rows
+    loc_ref[...] = jnp.dot(mt_all[...], pick.astype(jnp.float32),
+                           precision=lax.Precision.HIGHEST, preferred_element_type=jnp.float32)
+    load_own.wait()
+    factor_kernel(mt_all, own_ref, valid_ref, spread_ref, l_ref, inv_ref, w_ref, hi_ref, mid_ref, lo_ref)
+    load_vis.wait()
+    load_mine.wait()
 
     def copy(stage, src, dst, slot, peer, at):
         return pltpu.make_async_remote_copy(
             src_ref=src, dst_ref=dst, send_sem=sems.at[2 * stage, slot], recv_sem=sems.at[2 * stage + 1, at],
             device_id={"chan": peer}, device_id_type=MESH)
-
-    mate = chip * 2 + 1 - core
 
     def project(owner, dst, slot):
         for j in range(columns // LANES):
@@ -94,34 +141,36 @@
             at = pl.multiple_of(owner * width + 2 * j * LANES, 2 * LANES)
             v = vis_ref[:, pl.ds(at, 2 * LANES)] * w
             dst[slot, :, 2 * j * LANES : 2 * (j + 1) * LANES] = jnp.dot(
-                mt_ref[...], v, precision=lax.Precision.HIGHEST, preferred_element_type=jnp.float32)
-
-    def theirs(d, carry):
-        slot = lax.rem(chip + d, chips)
-        project(slot * 2 + 1 - core, give, slot)
-        copy(0, give.at[slot], take.at[slot], slot, mate, slot).start()
-        return carry
-
-    lax.fori_loop(1, chips + 1, theirs, 0)
-
-    def mine(d, carry):
-        slot = lax.rem(chip + d, chips)
-        project(slot * 2 + core, keep, slot)
-        return carry
-
-    lax.fori_loop(1, chips + 1, mine, 0)
-    for d in range(1, chips + 1):
-        slot = lax.rem(chip + d, chips)
-        copy(0, give.at[slot], take.at[slot], slot, mate, slot).wait()
-        if d < chips:
-            sums[slot] = keep[slot] + take[slot]
-            copy(1, sums.at[slot], come.at[chip], slot, slot * 2 + core, chip).start()
+                loc_ref[...], v, precision=lax.Precision.HIGHEST, preferred_element_type=jnp.float32)
+
+    flags(mate, mate, mate).wait_recv()
+    project(mate, give, chip)
+    pair = copy(0, give.at[chip], take.at[chip], chip, mate, chip)
+    pair.start()
+    project(me, keep, chip)
+    pair.wait()
+
+    def collect(d, carry):
+        slot = other(d)
+        first, second = slot * 2 + 1 - core, slot * 2 + core
+        flags(first, first, first).wait_recv()
+        project(first, give, slot)
+        pair = copy(0, give.at[slot], take.at[slot], slot, mate, slot)
+        pair.start()
+        flags(second, second, second).wait_recv()
+        project(second, keep, slot)
+        pair.wait()
+        sums[slot] = keep[slot] + take[slot]
+        copy(1, sums.at[slot], come.at[chip], slot, slot * 2 + core, chip).start()
+        return carry
+
+    lax.fori_loop(1, chips, collect, 0)
     total = keep[chip] + take[chip]
     for d in range(1, chips):
-        slot = lax.rem(chip + d, chips)
+        slot = other(d)
         copy(1, sums.at[slot], come.at[slot], slot, slot * 2 + core, slot).wait()
         total = total + come[slot]
-    take[chip] = total * valid_ref[...]
+    take[chip] = total * wide_ref[...]
 
     part = 2 * LANES
 
@@ -172,57 +221,73 @@
         block = out_ref.at[slot * 2 + 1 - core]
         spread(slot).wait_send()
         copy(3, block, block, slot, mate, slot).wait_recv()
+    flags(mate, me, me).wait_send()
+    for d in range(1, chips):
+        flags(other(d) * 2 + core, me, me).wait_send()
+        flags(other(d) * 2 + 1 - core, me, me).wait_send()
+    for d in range(1, groups):
+        modes_copy(lax.rem(grp + d, groups), grp).wait_send()
+
+
+def pieces(x):
+    hi = x.astype(jnp.bfloat16)
+    rest = x - hi.astype(jnp.float32)
+    mid = rest.astype(jnp.bfloat16)
+    return hi, mid, (rest - mid.astype(jnp.float32)).astype(jnp.bfloat16)
 
 
 def residual_kernel(vis_ref, modes_ref, coef_ref, out_ref):
     width = coef_ref.shape[2]
+    hi, mid, lo = pieces(modes_ref[...])
+    left = jnp.concatenate([hi, hi, mid, mid, hi, lo], axis=0)
     for j in range(coef_ref.shape[0]):
         cols = slice(j * width, (j + 1) * width)
-        out_ref[:, cols] = vis_ref[:, cols] - jnp.dot(
-            modes_ref[...], coef_ref[j], precision=lax.Precision.HIGHEST, preferred_element_type=jnp.float32)
-
-
-def per_device(chan, visibility, interference_mask, valid_time_count, fit_modes):
+        hi, mid, lo = pieces(coef_ref[j])
+        right = jnp.concatenate([hi, mid, hi, mid, lo, hi], axis=0)
+        out_ref[:, cols] = vis_ref[:, cols] - lax.dot_general(
+            left, right, (((0,), (0,)), ((), ())), preferred_element_type=jnp.float32)
+
+
+def per_device(chan, groups, visibility, interference_mask, valid_time_count, fit_modes):
     rows, all_columns = visibility.shape
     freqs, columns = interference_mask.shape
-    modes = fit_modes.shape[1]
+    share, modes = fit_modes.shape
     base = valid_time_count.shape[0]
     times = columns // base
     width = 2 * columns
     chips = chan // 2
-    flags = lax.all_to_all(interference_mask.reshape(chan, rows, columns), "chan", 0, 0)
-    table = lax.all_gather(fit_modes, "grp", axis=0, tiled=True)
-    local = lax.dynamic_slice_in_dim(table, lax.axis_index("chan") * rows, rows, 0)
     within = (lax.broadcasted_iota(jnp.int32, (base, times), 1) < valid_time_count[:, None]).astype(jnp.float32)
     valid = within.reshape(1, columns)
     valid_wide = jnp.broadcast_to(within[:, None, :], (base, 2, times)).reshape(1, width)
     source = lax.broadcasted_iota(jnp.int32, (LANES, 2 * LANES), 0)
     column = lax.broadcasted_iota(jnp.int32, (LANES, 2 * LANES), 1)
     spread = (source == column // (2 * times) * times + column % times).astype(jnp.bfloat16)
-    f32 = jnp.float32
-    factor, inverse = pl.pallas_call(
-        factor_kernel,
-        out_shape=(jax.ShapeDtypeStruct((modes, modes, width), f32), jax.ShapeDtypeStruct((modes, width), f32)),
-        in_specs=[VMEM] * 4,
+    f32, bf16 = jnp.float32, jnp.bfloat16
+    block = pltpu.VMEM((chips, modes, width), f32)
+    anywhere = pl.BlockSpec(memory_space=pl.ANY)
+    coefficients, local = pl.pallas_call(
+        functools.partial(fit_kernel, chips, groups),
+        out_shape=(jax.ShapeDtypeStruct((chan, modes, width), f32), jax.ShapeDtypeStruct((modes, rows), f32)),
+        in_specs=[anywhere] * 2 + [VMEM] * 4,
         out_specs=(VMEM, VMEM),
-        scratch_shapes=[pltpu.VMEM((freqs, width), jnp.bfloat16)]
-        + [pltpu.VMEM((modes * modes, freqs), jnp.bfloat16)] * 3,
-        compiler_params=pltpu.CompilerParams(vmem_limit_bytes=40 << 20),
-        cost_estimate=pl.CostEstimate(flops=20 * 10**9, bytes_accessed=8 << 20, transcendentals=0),
-        name="factor",
-    )(table.T, interference_mask, valid, spread)
-    block = pltpu.VMEM((chips, modes, width), f32)
-    coefficients = pl.pallas_call(
-        functools.partial(fit_kernel, chips),
-        out_shape=jax.ShapeDtypeStruct((chan, modes, width), f32),
-        in_specs=[VMEM] * 7,
-        out_specs=VMEM,
-        scratch_shapes=[block] * 5 + [pltpu.SemaphoreType.DMA((8, chips))],
+        scratch_shapes=[
+            pltpu.VMEM((rows, all_columns), f32),
+            pltpu.VMEM((freqs, columns), jnp.int32),
+            pltpu.VMEM((chan, rows, columns), jnp.int32),
+            pltpu.VMEM((groups, modes, share), f32),
+            pltpu.VMEM((modes, freqs), f32),
+            pltpu.VMEM((freqs, width), bf16),
+        ]
+        + [pltpu.VMEM((modes * modes, freqs), bf16)] * 3
+        + [pltpu.VMEM((modes, modes, width), f32), pltpu.VMEM((modes, width), f32)]
+        + [block] * 5
+        + [pltpu.SemaphoreType.DMA((8, chips)), pltpu.SemaphoreType.DMA((2, chan)),
+           pltpu.SemaphoreType.DMA((2, groups)), pltpu.SemaphoreType.DMA((3,))],
         compiler_params=pltpu.CompilerParams(
-            collective_id=0, has_side_effects=True, vmem_limit_bytes=56 << 20),
+            collective_id=0, has_side_effects=True, vmem_limit_bytes=61 << 20),
         cost_estimate=pl.CostEstimate(flops=10**10, bytes_accessed=12 << 20, transcendentals=0),
         name="fit",
-    )(visibility, flags, local.T, spread, valid_wide, factor, inverse)
+    )(visibility, interference_mask, fit_modes.T, spread, valid, valid_wide)
     step = 2
     return pl.pallas_call(
         residual_kernel,
@@ -230,7 +295,7 @@
         out_shape=jax.ShapeDtypeStruct((rows, all_columns), f32),
         in_specs=[
             pl.BlockSpec((rows, step * width), lambda i: (0, i)),
-            pl.BlockSpec((rows, modes), lambda i: (0, 0)),
+            pl.BlockSpec((modes, rows), lambda i: (0, 0)),
             pl.BlockSpec((step, modes, width), lambda i: (i, 0, 0)),
         ],
         out_specs=pl.BlockSpec((rows, step * width), lambda i: (0, i)),
@@ -241,5 +306,5 @@
 def solution(mesh):
     placed = (P("chan", "grp"), P(None, ("grp", "chan")), P(("grp", "chan")), P("grp", None))
     return jax.shard_map(
-        functools.partial(per_device, mesh.shape["chan"]), mesh=mesh, in_specs=placed, out_specs=P("chan", "grp"),
-        check_vma=False)
+        functools.partial(per_device, mesh.shape["chan"], mesh.shape["grp"]), mesh=mesh, in_specs=placed,
+        out_specs=P("chan", "grp"), check_vma=False)

time: 101 us -> 86.2 us (0.85)
  Pallas kernels: 59.2 us -> 82.2 us
  waiting for transfers between devices: 19.1 us -> 0 us
  blocking collectives: 10.7 us -> 0 us
  starting transfers between devices: 6.5 us -> 0 us
  local copies, waits for them, and re-layouts: 5.01 us -> 1.35 us
  other arithmetic: 0.11 us -> 1.39 us
    pallas_call x2 -> x1, Pallas kernels: 52 us -> 76.6 us  [per_device(): pl.pallas_call(functools.partial(fit_kernel, chips, groups), out_shape=(j...]
    all_to_all x1 -> x0, waiting for transfers between devices: 19.1 us -> none  [per_device(): lax.all_to_all(interference_mask.reshape(chan, rows, columns), 'chan', 0, 0)]
    all_gather x1 -> x0, blocking collectives: 10.7 us -> none  [per_device(): table = lax.all_gather(fit_modes, 'grp', axis=0, tiled=True)]
    all_to_all x1 -> x0, starting transfers between devices: 6.5 us -> none  [per_device(): lax.all_to_all(interference_mask.reshape(chan, rows, columns), 'chan', 0, 0)]
    unnamed x13 -> x0, local copies, waits for them, and re-layouts: 2.76 us -> none
    pallas_call x1, Pallas kernels: 7.21 us -> 5.56 us  [per_device(): pl.pallas_call(residual_kernel, grid=(chan // step,), out_shape=jax.Shape...]
  transfers between devices with their start and end apart: 1 -> 0, of which waited for: 1 -> 0; matrix products, arithmetic and copies ran while one was open for 2% -> 0% of each run, Pallas kernels for 14% -> 0%
where the time goes in v2:
time: 86.2 us; the launch traced here: 85 us
  Pallas kernels  82.2 us (95%)
  other arithmetic  1.39 us (2%)
  local copies, waits for them, and re-layouts  1.35 us (2%)
    pallas_call x1, Pallas kernels, per_device(): pl.pallas_call(functools.partial(fit_kernel, chips, groups), out_shape=(j...  76.6 us
    pallas_call x1, Pallas kernels, per_device(): pl.pallas_call(residual_kernel, grid=(chan // step,), out_shape=jax.Shape...  5.56 us

profile of v2, /device:TPU:0, one launch (start us, length us, event | category | flops | bytes accessed | tf_op | source)
XLA Modules:
  0.0 85.0 jit_solution(14063311493966044461)
XLA Ops:
  0.0 0.7 fusion.1
  0.8 0.7 reshape.47.valid_ref
  1.4 0.7 reshape.46.wide_ref
  2.1 0.6 fusion.spread_ref
  2.7 76.6 %fit.1 = (f32[8,32,1024]{2,1,0:T(8,128)}, f32[32,128]{1,0:T(8,128)}) custom-call(f32[128,8192]{1,0:T(8,128)} %vis_ref.1, s32[1024,512]{1,0:T(8,128)} %mask_hbm.1, f32[32,256]{1,0:T(8,128)} %bitcast.1, bf16[128,256]{1,0:T(8,128)(2,1)} %fusion.spread_ref, f32[1,512]{1,0:T(1,128)} %reshape.47.valid_ref, f32[1,1024]{1,0:T(1,128)} %reshape.46.wide_ref), custom_call_target="tpu_custom_call" | custom-call | flops 10000000000 | bytes 12582912 | tf_op jit(solution)/shard_map/fit/pallas_call | solution.py:268
  79.4 5.6 %residual.1 = f32[128,8192]{1,0:T(8,128)} custom-call(f32[128,8192]{1,0:T(8,128)} %vis_ref.1, f32[32,128]{1,0:T(8,128)} %get-tuple-element.7.modes_ref, f32[8,32,1024]{2,1,0:T(8,128)} %get-tuple-element.8.coef_ref), custom_call_target="tpu_custom_call" | custom-call | tf_op jit(solution)/shard_map/residual/pallas_call | solution.py:292
  (4 shorter events, 0.0 us)
